TPU v7x, 32 devices: a whole 2x2x4 slice. The times are simulated.
32 devices in a mesh: replica: 2 (over y), expert: 8 (over z, core), tensor: 2 (over x).
Axes of the slice: x: 2, y: 2, z: 4, core: 2. Of those that a mesh axis runs over, the one named last changes fastest.
Arguments:
- delta: bfloat16 [2, 128, 4, 14336], P('replica', 'expert', None, 'tensor'), may hold values from -6 to 6
- step_offsets: int32 [2], replicated, may hold values from 0 to 15, as said below
- block_map: int32 [128], replicated, may hold values from 0 to 127, as said below
- master_params: float32 [128, 4, 14336], P('expert', 'replica', 'tensor'), may hold values from -6 to 6
- first_moment: float32 [128, 4, 14336], P('expert', 'replica', 'tensor'), may hold values from -2 to 2
- second_moment: float32 [128, 4, 14336], P('expert', 'replica', 'tensor'), may hold values from 0.01 to 1
Outputs:
- new_params: bfloat16 [128, 4, 14336], P('expert', 'replica')
- new_first: float32 [128, 4, 14336], P('expert', 'replica', 'tensor')
- new_second: float32 [128, 4, 14336], P('expert', 'replica', 'tensor')
Inputs may be any that keep to these rules, and one draw needn't show every extreme that they name: `block_map`: A permutation of the block indices onto owner slots; slot s belongs to expert index s // 16, and the blocks b with b // 16 = i go in equal numbers to every expert index. `step_offsets`: the replica groups' offsets are distinct.
All inputs are finite; a program needn't handle non-finite values.
Results may differ from a plain program's by a relative error of at most 0.0035.
Values may be sent and summed in bfloat16 or wider, within the bound.
A program may use at most 64 MiB of HBM per device.

v0:
```python
import jax
import jax.numpy as jnp
from jax import lax
from jax.sharding import PartitionSpec as P

beta_one = 0.9
beta_two = 0.99
outer_rate = 0.7
outer_round = 20
epsilon = 1e-08


def replica_weights(step_offsets):
    reciprocal = 1.0 / (1.0 + step_offsets.astype(jnp.float32))
    return reciprocal / jnp.sum(reciprocal)


def adam_update(gradient, master_params, first_moment, second_moment):
    new_first = beta_one * first_moment + (1.0 - beta_one) * gradient
    new_second = beta_two * second_moment + (1.0 - beta_two) * gradient * gradient
    fix_one = 1.0 - beta_one**outer_round
    fix_two = 1.0 - beta_two**outer_round
    update_step = new_first / fix_one / (jnp.sqrt(new_second / fix_two) + epsilon)
    new_params = (master_params - outer_rate * update_step).astype(jnp.bfloat16)
    return (new_params, new_first, new_second)


def body(delta, step_offsets, block_map, master_params, first_moment, second_moment):
    blocks = delta.shape[1]
    rows_all = delta.shape[2]
    columns = delta.shape[3]
    my_expert = lax.axis_index("expert")
    weights = replica_weights(step_offsets)
    own_weight = weights[lax.axis_index("replica")]
    weighted = (delta[0].astype(jnp.float32) * own_weight).astype(jnp.bfloat16)
    local_map = lax.dynamic_slice_in_dim(block_map, my_expert * blocks, blocks)
    local_ids = jnp.arange(blocks, dtype=jnp.int32)
    sort_order = jnp.argsort(local_map // blocks * blocks + local_ids)
    total_blocks = block_map.shape[0]
    every_id = jnp.arange(total_blocks, dtype=jnp.int32)
    ranked = jnp.where(block_map // blocks == my_expert, every_id, total_blocks + every_id)
    picked = jnp.argsort(ranked)[:blocks]
    placement_ids = jnp.argsort(block_map[picked] % blocks)
    flat_terms = weighted.reshape(blocks, rows_all * columns)
    partial_value = lax.psum_scatter(flat_terms, "replica", scatter_dimension=1, tiled=True).astype(
        jnp.float32
    )
    outgoing = partial_value[sort_order]
    arrived = lax.all_to_all(
        outgoing.astype(jnp.bfloat16), "expert", split_axis=0, concat_axis=0, tiled=True
    ).astype(outgoing.dtype)
    summed = arrived[placement_ids]
    gradient = summed.reshape(master_params.shape)
    new_params, new_first, new_second = adam_update(
        gradient, master_params, first_moment, second_moment
    )
    full_params = lax.all_gather(new_params, "tensor", axis=2, tiled=True)
    return (full_params, new_first, new_second)


def solution(mesh):
    in_specs = (
        P("replica", "expert", None, "tensor"),
        P(),
        P(),
        P("expert", "replica", "tensor"),
        P("expert", "replica", "tensor"),
        P("expert", "replica", "tensor"),
    )
    out_specs = (
        P("expert", "replica", None),
        P("expert", "replica", "tensor"),
        P("expert", "replica", "tensor"),
    )
    return jax.shard_map(body, mesh=mesh, in_specs=in_specs, out_specs=out_specs, check_vma=False)
```

profile of v0, /device:TPU:0, one launch (start us, length us, event | category | flops | bytes accessed | tf_op | source)
XLA Modules:
  0.0 84.9 jit_solution(8649354301705152632)
XLA Ops:
  7.2 0.0 reduce-scatter.2.cloned.1.call-start
  7.2 1.3 %divide_reduce_fusion = f32[]{:T(128)} fusion(s32[2]{0:T(128)} %param.7), kind=kLoop, calls=%fused_computation.30 | loop fusion | flops 7 | bytes 12 | tf_op jit(solution)/shard_map/reduce_sum | solution.py:15
  8.5 1.3 %multiply_divide_fusion = f32[2]{0:T(128)S(1)} fusion(s32[2]{0:T(128)} %param.7, f32[]{:T(128)} %divide_reduce_fusion), kind=kLoop, calls=%fused_computation.29 | loop fusion | flops 8 | bytes 20 | tf_op jit(solution)/shard_map/div | solution.py:15
  9.8 0.6 dynamic_slice.6
  10.4 2.2 %multiply_convert_fusion = bf16[1,16,4,7168]{3,2,1,0:T(4,128)(2,1)S(1)} fusion(bf16[1,16,4,7168]{3,2,1,0:T(4,128)(2,1)} %param.6, f32[]{:T(128)} %bitcast), kind=kLoop, calls=%fused_computation.3 | loop fusion | flops 1376256 | bytes 1835012 | tf_op jit(solution)/shard_map/convert_element_type | solution.py:35
  12.6 1.2 %copy.9 = bf16[2,8,4,7168]{3,1,2,0:T(8,128)(2,1)} copy(bf16[2,8,4,7168]{3,2,1,0:T(4,128)(2,1)S(1)} %bitcast.5) | data formatting | bytes 1835008
  13.8 0.0 copy-start
  13.8 0.0 reduce-scatter.2.cloned.1.call-update
  13.8 0.6 copy-done
  14.4 2.5 %sort.49 = (s32[128]{0:T(128)}, s32[128]{0:T(128)S(1)}) sort(s32[128]{0:T(128)S(1)} %compare_select_fusion.5, s32[128]{0:T(128)S(1)} %iota.23), dimensions={0}, to_apply=%region_3.4 | sort | flops 896 | bytes 2048 | tf_op jit(solution)/shard_map/jit(argsort)/sort | solution.py:42
  17.0 0.1 iota_add_fusion
  17.1 1.2 %sort.48 = (s32[16]{0:T(128)}, s32[16]{0:T(128)S(1)}) sort(s32[16]{0:T(128)S(1)} %iota_add_fusion, s32[16]{0:T(128)S(1)} %iota.20), dimensions={0}, to_apply=%region_2.3 | sort | flops 64 | bytes 256 | tf_op jit(solution)/shard_map/jit(argsort)/sort | solution.py:38
  18.3 17.3 %reduce-scatter.2.cloned.1.call-done = bf16[16,14336]{1,0:T(8,128)(2,1)} async-done(((bf16[16,28672]{1,0:T(8,128)(2,1)}), bf16[16,14336]{1,0:T(8,128)(2,1)}) %reduce-scatter.2.cloned.1.call-update) | async-done | bytes 458768 | tf_op jit(solution)/shard_map/reduce_scatter | solution.py:45
  35.6 2.3 %gather_fusion = bf16[16,14336]{1,0:T(8,128)(2,1)S(1)} fusion(bf16[16,14336]{1,0:T(8,128)(2,1)} %reduce-scatter.2.cloned.1.call-done, s32[1024]{0:T(1024)S(1)} %pad_clamp_fusion.2), kind=kCustom, calls=%fused_computation | custom fusion | bytes 917568 | tf_op jit(solution)/shard_map/gather | solution.py:48
  37.9 1.1 %convert_element_type.40 = bf16[8,2,14336]{2,1,0:T(2,128)(2,1)} reshape(bf16[16,14336]{1,0:T(8,128)(2,1)S(1)} %gather_fusion) | data formatting | bytes 917504 | tf_op jit(solution)/shard_map/convert_element_type | solution.py:50
  39.0 4.6 %all-to-all-start = ((bf16[8,2,14336]{2,1,0:T(2,128)(2,1)}), bf16[8,2,14336]{2,1,0:T(2,128)(2,1)S(1)}, u32[]{:S(2)}, u32[]{:S(2)}) async-start(bf16[8,2,14336]{2,1,0:T(2,128)(2,1)} %convert_element_type.40), calls=%async_computation.1 | async-start | bytes 917504 | tf_op jit(solution)/shard_map/all_to_all | solution.py:49
  43.7 0.7 gather_fusion.1
  44.3 1.3 %sort.50 = (s32[16]{0:T(128)}, s32[16]{0:T(128)S(1)}) sort(s32[16]{0:T(128)S(1)} %and_select_fusion, s32[16]{0:T(128)S(1)} %iota.24), dimensions={0}, to_apply=%region_4.5 | sort | flops 64 | bytes 256 | tf_op jit(solution)/shard_map/jit(argsort)/sort | solution.py:43
  45.6 12.0 %all-to-all-done = bf16[8,2,14336]{2,1,0:T(2,128)(2,1)S(1)} async-done(((bf16[8,2,14336]{2,1,0:T(2,128)(2,1)}), bf16[8,2,14336]{2,1,0:T(2,128)(2,1)S(1)}, u32[]{:S(2)}, u32[]{:S(2)}) %all-to-all-start) | async-done | bytes 458784 | tf_op jit(solution)/shard_map/all_to_all | solution.py:49
  57.6 0.1 reshape.22
  57.7 0.8 %gather_fusion.2 = f32[16,14336]{1,0:T(8,128)S(1)} fusion(f32[16,14336]{1,0:T(8,128)S(1)} %reshape.22, s32[1024]{0:T(1024)S(1)} %pad_clamp_fusion), kind=kCustom, calls=%fused_computation.2 | custom fusion | bytes 1835072 | tf_op jit(solution)/shard_map/gather | solution.py:52
  58.5 0.0 copy-start.1
  58.6 0.8 reshape.21
  59.3 0.4 copy-done.1
  59.7 4.8 %subtract_convert_fusion = (bf16[16,2,7168]{2,1,0:T(2,128)(2,1)S(1)}, f32[16,2,7168]{2,1,0:T(2,128)}, f32[16,2,7168]{2,1,0:T(2,128)}) fusion(f32[16,2,7168]{2,1,0:T(2,128)S(1)} %copy-done.1, f32[16,2,7168]{2,1,0:T(2,128)S(1)} %reshape.21, f32[16,2,7168]{2,1,0:T(2,128)} %param.10, f32[16,2,7168]{2,1,0:T(2,128)} %param.11), kind=kLoop, calls=%fused_computation.6 | loop fusion | flops 3211264 | bytes 5963776 | tf_op jit(solution)/shard_map/convert_element_type | solution.py:24
  64.6 12.6 %all_gather.3 = bf16[16,2,14336]{2,1,0:T(2,128)(2,1)S(1)} all-gather(bf16[16,2,7168]{2,1,0:T(2,128)(2,1)S(1)} %get-tuple-element.9), channel_id=1, replica_groups=mesh['replica'=2,'expert'=8,'tensor'=2] {'tensor'}, dimensions={2}, use_global_device_ids=true | all-gather | bytes 1376256 | tf_op jit(solution)/shard_map/all_gather | solution.py:57
  77.2 0.9 %copy.11 = bf16[16,2,14336]{2,1,0:T(2,128)(2,1)} copy(bf16[16,2,14336]{2,1,0:T(2,128)(2,1)S(1)} %all_gather.3) | data formatting | bytes 1835008
  (11 shorter events, 0.1 us)
Async XLA Ops:
  7.2 28.5 %reduce-scatter.2.cloned.1.call-start = ((), (), s32[]{:S(2)}) async-start(), calls=%async_computation.2 | async-start | bytes 1376256 | tf_op jit(solution)/shard_map/reduce_scatter | solution.py:45
  13.8 0.7 copy-start
  39.0 18.5 %all-to-all-start = ((bf16[8,2,14336]{2,1,0:T(2,128)(2,1)}), bf16[8,2,14336]{2,1,0:T(2,128)(2,1)S(1)}, u32[]{:S(2)}, u32[]{:S(2)}) async-start(bf16[8,2,14336]{2,1,0:T(2,128)(2,1)} %convert_element_type.40), calls=%async_computation.1 | async-start | bytes 917504 | tf_op jit(solution)/shard_map/all_to_all | solution.py:49
  58.5 1.2 %copy-start.1 = (f32[16,2,7168]{2,1,0:T(2,128)S(1)}, f32[16,2,7168]{2,1,0:T(2,128)}, u32[]{:S(2)}) copy-start(f32[16,2,7168]{2,1,0:T(2,128)} %param.9) | copy-start | bytes 2752516
Sparse Core Ops, SparseCore 0:
  13.9 21.6 reduce-scatter.1
where the time goes:
time: 85.3 us; the launch traced here: 84.9 us
  waiting for transfers between devices  29.3 us (34%)
  other arithmetic  14.8 us (17%)
  between operations  14.1 us (17%)
  blocking collectives  12.6 us (15%)
  local copies, waits for them, and re-layouts  9.52 us (11%)
  starting transfers between devices  4.66 us (5%)
    reduce_scatter x1, waiting for transfers between devices, body(): lax.psum_scatter(flat_terms, 'replica', scatter_dimension=1, tiled=True)  17.3 us
    all_gather x1, blocking collectives, body(): full_params = lax.all_gather(new_params, 'tensor', axis=2, tiled=True)  12.6 us
    all_to_all x1, waiting for transfers between devices, body(): lax.all_to_all(outgoing.astype(jnp.bfloat16), 'expert', split_axis=0, con...  12 us
    convert_element_type x1, other arithmetic, adam_update(): new_params = (master_params - outer_rate * update_step).astype(jnp.bfloat16)  4.83 us
    all_to_all x1, starting transfers between devices, body(): lax.all_to_all(outgoing.astype(jnp.bfloat16), 'expert', split_axis=0, con...  4.62 us
    unnamed x6, local copies, waits for them, and re-layouts  3.13 us
    sort x1, other arithmetic, body(): picked = jnp.argsort(ranked)[:blocks]  2.54 us
    gather x1, local copies, waits for them, and re-layouts, body(): outgoing = partial_value[sort_order]  2.31 us
  transfers between devices with their start and end apart: 2, of which 2 were waited for; matrix products, arithmetic and copies ran while one was open for 7% of the time, Pallas kernels for 0%

commit v1 on v0

v1 whole, which is shorter than its diff:
```python
import functools

import jax
import jax.numpy as jnp
from jax import lax
from jax.experimental import pallas as pl
from jax.experimental.pallas import tpu as pltpu
from jax.sharding import PartitionSpec as P

beta_one = 0.9
beta_two = 0.99
outer_rate = 0.7
outer_round = 20
epsilon = 1e-08

LANES = 128
CHUNK = 8
LAG = 3
UNROLL = 4
MESH = pl.DeviceIdType.MESH


def kernel(
    sizes,
    block_map,
    step_offsets,
    delta,
    master_params,
    first_moment,
    second_moment,
    out_params,
    out_first,
    out_second,
    master,
    first,
    second,
    params,
    new_first,
    new_second,
    order,
    slots,
    places,
    load_sem,
    state_sem,
    own_sem,
    store_sem,
    y_send,
    y_recv,
    z_send,
    z_recv,
    x_send,
    x_recv,
    *buffers,
):
    replicas, experts, tensors, chunks, blocks, pairs, rows = sizes
    count = len(chunks)
    stage = buffers[:count]
    arrived = buffers[count : 2 * count]
    outgoing = buffers[2 * count : 3 * count]
    incoming = buffers[3 * count :]
    my_replica = lax.axis_index("replica")
    my_expert = lax.axis_index("expert")
    my_tensor = lax.axis_index("tensor")
    columns = sum(chunks)
    starts = [sum(chunks[:c]) for c in range(count)]

    def load(c, d):
        replica = lax.rem(my_replica + d, replicas)
        return pltpu.make_async_copy(
            delta.at[:, pl.ds(starts[c], chunks[c]), replica],
            stage[c].at[d],
            load_sem.at[c, d],
        )

    def y_copy(c, d):
        return pltpu.make_async_remote_copy(
            src_ref=stage[c].at[d],
            dst_ref=arrived[c].at[d - 1],
            send_sem=y_send.at[c, d],
            recv_sem=y_recv.at[c, d],
            device_id={"replica": lax.rem(my_replica + d, replicas)},
            device_id_type=MESH,
        )

    def z_copy(c, d):
        peer = lax.rem(my_expert + d, experts)
        return pltpu.make_async_remote_copy(
            src_ref=outgoing[c].at[pl.ds(peer * pairs, pairs)],
            dst_ref=incoming[c].at[pl.ds(my_expert * pairs, pairs)],
            send_sem=z_send.at[c, d],
            recv_sem=z_recv.at[c, d],
            device_id={"expert": peer},
            device_id_type=MESH,
        )

    def z_own(c):
        mine = pl.ds(my_expert * pairs, pairs)
        return pltpu.make_async_copy(outgoing[c].at[mine], incoming[c].at[mine], own_sem.at[c])

    def x_copy(c, d):
        part = params.at[:, pl.ds(my_tensor * columns + starts[c], chunks[c])]
        return pltpu.make_async_remote_copy(
            src_ref=part,
            dst_ref=part,
            send_sem=x_send.at[c, d],
            recv_sem=x_recv.at[c, d],
            device_id={"tensor": lax.rem(my_tensor + d, tensors)},
            device_id_type=MESH,
        )

    def store(c, which):
        held, out = ((new_first, out_first), (new_second, out_second))[which]
        part = pl.ds(starts[c] * rows, chunks[c] * rows)
        return pltpu.make_async_copy(held.at[:, part], out.at[:, part], store_sem.at[c, which])

    barrier = pltpu.get_barrier_semaphore()
    axes = (("replica", my_replica, replicas), ("expert", my_expert, experts), ("tensor", my_tensor, tensors))
    for axis, mine, size in axes:
        for d in range(1, size):
            pl.semaphore_signal(
                barrier, inc=1, device_id={axis: lax.rem(mine + d, size)}, device_id_type=MESH
            )
    for c in range(count):
        for d in list(range(1, replicas)) + [0]:
            load(c, d).start()
    states = [
        pltpu.make_async_copy(source, held, state_sem.at[i])
        for i, (source, held) in enumerate(
            ((master_params, master), (first_moment, first), (second_moment, second))
        )
    ]
    for copy in states:
        copy.start()

    def note_order(e, carry):
        seen = jnp.int32(0)
        found = [jnp.int32(0)] * pairs
        for j in range(blocks):
            owned = lax.div(block_map[my_expert * blocks + j], jnp.int32(blocks)) == e
            for k in range(pairs):
                found[k] = jnp.where(owned, jnp.where(seen == k, j, found[k]), found[k])
            seen = seen + jnp.where(owned, 1, 0)
        for k in range(pairs):
            order[e * pairs + k] = found[k]
        return carry

    def note_slots(i, carry):
        seen = jnp.int32(0)
        found = [jnp.int32(0)] * pairs
        for j in range(blocks):
            slot = block_map[i * blocks + j] - my_expert * blocks
            owned = jnp.where(slot >= 0, jnp.where(slot < blocks, 1, 0), 0)
            for k in range(pairs):
                found[k] = jnp.where(owned == 1, jnp.where(seen == k, slot, found[k]), found[k])
            seen = seen + owned
        for k in range(pairs):
            slots[i * pairs + k] = found[k]
        return carry

    def note_places(s, carry):
        place = jnp.int32(0)
        for q in range(blocks):
            place = jnp.where(slots[q] == s, q, place)
        places[s] = place
        return carry

    lax.fori_loop(0, experts, note_order, 0)
    lax.fori_loop(0, experts, note_slots, 0)
    lax.fori_loop(0, blocks, note_places, 0)

    pl.semaphore_wait(barrier, replicas + experts + tensors - 3)
    for c in range(count):
        for d in range(1, replicas):
            load(c, d).wait()
            y_copy(c, d).start()

    shares = [
        1.0 / jnp.full((8, LANES), 1 + step_offsets[lax.rem(my_replica + replicas - d, replicas)], jnp.int32).astype(jnp.float32)
        for d in range(replicas)
    ]
    total = functools.reduce(lambda a, b: a + b, shares)
    weights = [(share / total)[:1] for share in shares]

    fix_one = 1.0 - beta_one**outer_round
    fix_two = 1.0 - beta_two**outer_round

    def add_up(c):
        load(c, 0).wait()
        for d in range(1, replicas):
            y_copy(c, d).wait_recv()
        dense = chunks[c] * rows
        own = stage[c].reshape(replicas, blocks, dense, LANES)
        others = arrived[c].reshape(replicas - 1, blocks, dense, LANES)
        out = outgoing[c].reshape(blocks, dense, LANES)

        def step(n, carry):
            for u in range(UNROLL):
                p = n * UNROLL + u
                block = order[p]
                value = own[0, block].astype(jnp.float32) * weights[0]
                for d in range(1, replicas):
                    value = value + others[d - 1, block].astype(jnp.float32) * weights[d]
                out[p] = value.astype(jnp.bfloat16)
            return carry

        lax.fori_loop(0, blocks // UNROLL, step, 0)

    def adam(c):
        dense = chunks[c] * rows
        terms = incoming[c].reshape(blocks, dense, LANES)
        held = params.reshape(blocks, tensors * columns * rows, LANES)
        part = pl.ds(starts[c] * rows, dense)
        target = pl.ds(pl.multiple_of((my_tensor * columns + starts[c]) * rows, 16), dense)

        def step(n, carry):
            for u in range(UNROLL):
                s = n * UNROLL + u
                gradient = terms[places[s]].astype(jnp.float32)
                one = beta_one * first[s, part] + (1.0 - beta_one) * gradient
                two = beta_two * second[s, part] + (1.0 - beta_two) * gradient * gradient
                new_first[s, part] = one
                new_second[s, part] = two
                update = (outer_rate / fix_one) * one / (jnp.sqrt(two * (1.0 / fix_two)) + epsilon)
                held[s, target] = (master[s, part] - update).astype(jnp.bfloat16)
            return carry

        lax.fori_loop(0, blocks // UNROLL, step, 0)

    def finish(c):
        if c == 0:
            for copy in states:
                copy.wait()
        z_own(c).wait()
        for d in range(1, experts):
            z_copy(c, d).wait_recv()
        adam(c)
        for d in range(1, tensors):
            x_copy(c, d).start()
        for which in range(2):
            store(c, which).start()

    for c in range(count):
        add_up(c)
        for d in range(1, experts):
            z_copy(c, d).start()
        z_own(c).start()
        if c >= LAG:
            finish(c - LAG)
    for c in range(max(count - LAG, 0), count):
        finish(c)

    for c in range(count):
        for d in range(1, replicas):
            y_copy(c, d).wait_send()
        for d in range(1, experts):
            z_copy(c, d).wait_send()
        for which in range(2):
            store(c, which).wait()
    for c in range(count):
        for d in range(1, tensors):
            x_copy(c, d).wait()
    last = pltpu.make_async_copy(params, out_params, state_sem.at[0])
    last.start()
    last.wait()


def body(delta, step_offsets, block_map, master_params, first_moment, second_moment, *, shape):
    replicas, experts, tensors = shape
    blocks, rows_all, width = delta.shape[1:]
    rows = rows_all // replicas
    columns = width // LANES
    pairs = blocks // experts
    chunks = [CHUNK] * (columns // CHUNK)
    count = len(chunks)
    terms = delta.reshape(blocks, replicas, rows, columns, LANES).transpose(0, 3, 1, 2, 4)

    def dense(state):
        split = state.reshape(blocks, rows, columns, LANES).transpose(0, 2, 1, 3)
        return split.reshape(blocks, columns * rows, LANES)

    def undense(state):
        split = state.reshape(blocks, columns, rows, LANES).transpose(0, 2, 1, 3)
        return split.reshape(blocks, rows, width)

    state_shape = (blocks, columns * rows, LANES)
    params_shape = (blocks, tensors * columns, rows, LANES)
    anywhere = pl.BlockSpec(memory_space=pl.ANY)
    scalars = pl.BlockSpec(memory_space=pltpu.SMEM)
    dma = pltpu.SemaphoreType.DMA
    sizes = (replicas, experts, tensors, chunks, blocks, pairs, rows)
    new_params, new_first, new_second = pl.pallas_call(
        functools.partial(kernel, sizes),
        out_shape=(
            jax.ShapeDtypeStruct(params_shape, jnp.bfloat16),
            jax.ShapeDtypeStruct(state_shape, jnp.float32),
            jax.ShapeDtypeStruct(state_shape, jnp.float32),
        ),
        in_specs=[scalars] * 2 + [anywhere] * 4,
        out_specs=(anywhere,) * 3,
        scratch_shapes=[
            pltpu.VMEM(state_shape, jnp.float32),
            pltpu.VMEM(state_shape, jnp.float32),
            pltpu.VMEM(state_shape, jnp.float32),
            pltpu.VMEM(params_shape, jnp.bfloat16),
            pltpu.VMEM(state_shape, jnp.float32),
            pltpu.VMEM(state_shape, jnp.float32),
            pltpu.SMEM((blocks,), jnp.int32),
            pltpu.SMEM((blocks,), jnp.int32),
            pltpu.SMEM((blocks,), jnp.int32),
            dma((count, replicas)),
            dma((3,)),
            dma((count,)),
            dma((count, 2)),
            dma((count, replicas)),
            dma((count, replicas)),
            dma((count, experts)),
            dma((count, experts)),
            dma((count, tensors)),
            dma((count, tensors)),
        ]
        + [pltpu.VMEM((replicas, blocks, c, rows, LANES), jnp.bfloat16) for c in chunks]
        + [pltpu.VMEM((replicas - 1, blocks, c, rows, LANES), jnp.bfloat16) for c in chunks]
        + [pltpu.VMEM((blocks, c, rows, LANES), jnp.bfloat16) for c in chunks]
        + [pltpu.VMEM((blocks, c, rows, LANES), jnp.bfloat16) for c in chunks],
        compiler_params=pltpu.CompilerParams(collective_id=0, has_side_effects=True),
    )(block_map, step_offsets, terms, dense(master_params), dense(first_moment), dense(second_moment))
    full = new_params.transpose(0, 2, 1, 3).reshape(blocks, rows, tensors * width)
    return (full, undense(new_first), undense(new_second))


def solution(mesh):
    in_specs = (
        P("replica", "expert", None, "tensor"),
        P(),
        P(),
        P("expert", "replica", "tensor"),
        P("expert", "replica", "tensor"),
        P("expert", "replica", "tensor"),
    )
    out_specs = (
        P("expert", "replica", None),
        P("expert", "replica", "tensor"),
        P("expert", "replica", "tensor"),
    )
    shape = tuple(mesh.shape[axis] for axis in ("replica", "expert", "tensor"))
    step = functools.partial(body, shape=shape)
    return jax.shard_map(step, mesh=mesh, in_specs=in_specs, out_specs=out_specs, check_vma=False)
```

time: 85.3 us -> 36 us (0.42)
  Pallas kernels: 0 us -> 29.9 us
  waiting for transfers between devices: 29.3 us -> 0 us
  other arithmetic: 14.8 us -> 0 us
  between operations: 14.1 us -> 0.65 us
  blocking collectives: 12.6 us -> 0 us
  starting transfers between devices: 4.66 us -> 0 us
  local copies, waits for them, and re-layouts: 9.52 us -> 5.25 us
    pallas_call x0 -> x1, Pallas kernels: none -> 29.9 us  [body(): pl.pallas_call(functools.partial(kernel, sizes), out_shape=(jax.ShapeDtyp...]
    reduce_scatter x1 -> x0, waiting for transfers between devices: 17.3 us -> none  [body(): lax.psum_scatter(flat_terms, 'replica', scatter_dimension=1, tiled=True)]
    all_gather x1 -> x0, blocking collectives: 12.6 us -> none  [body(): full_params = lax.all_gather(new_params, 'tensor', axis=2, tiled=True)]
    all_to_all x1 -> x0, waiting for transfers between devices: 12 us -> none  [body(): lax.all_to_all(outgoing.astype(jnp.bfloat16), 'expert', split_axis=0, con...]
    convert_element_type x2 -> x0, other arithmetic: 7.01 us -> none  [the longest x1 4.83 us: adam_update(): new_params = (master_params - outer_rate * update_step).astype(jnp.bfloat16)]
    sort x3 -> x0, other arithmetic: 5.03 us -> none  [the longest x1 2.54 us: body(): picked = jnp.argsort(ranked)[:blocks]]
    all_to_all x1 -> x0, starting transfers between devices: 4.62 us -> none  [body(): lax.all_to_all(outgoing.astype(jnp.bfloat16), 'expert', split_axis=0, con...]
    gather x3 -> x0, local copies, waits for them, and re-layouts: 3.82 us -> none  [the longest x1 2.31 us: body(): outgoing = partial_value[sort_order]]
  transfers between devices with their start and end apart: 2 -> 0, of which waited for: 2 -> 0; matrix products, arithmetic and copies ran while one was open for 7% -> 0% of each run, Pallas kernels for 0% -> 0%
where the time goes in v1:
time: 36 us; the launch traced here: 35.8 us
  Pallas kernels  29.9 us (83%)
  local copies, waits for them, and re-layouts  5.25 us (15%)
  between operations  0.65 us (2%)
    pallas_call x1, Pallas kernels, body(): pl.pallas_call(functools.partial(kernel, sizes), out_shape=(jax.ShapeDtyp...  29.9 us
    unnamed x7, local copies, waits for them, and re-layouts  5.25 us

profile of v1, /device:TPU:0, one launch (start us, length us, event | category | flops | bytes accessed | tf_op | source)
XLA Modules:
  0.0 35.8 jit_solution(14070283619283198079)
XLA Ops:
  0.6 29.9 %shard_map.85 = (bf16[16,112,2,128]{3,2,1,0:T(2,128)(2,1)}, f32[16,112,128]{2,1,0:T(8,128)}, f32[16,112,128]{2,1,0:T(8,128)}) custom-call(s32[128]{0:T(128)} %block_map.1, s32[2]{0:T(128)} %step_offsets.1, bf16[16,56,2,2,128]{4,3,2,1,0:T(2,128)(2,1)} %bitcast.34, f32[16,112,128]{2,1,0:T(8,128)} %bitcast.35, f32[16,112,128]{2,1,0:T(8,128)} %bitcast.36, ...), custom_call_target="tpu_custom_call" | custom-call | tf_op jit(solution)/shard_map/pallas_call | solution.py:291
  30.6 0.0 copy-start.1
  30.6 2.8 %copy.17 = bf16[16,2,14336]{2,1,0:T(2,128)(2,1)} copy(bf16[16,2,14336]{2,1,0:T(2,128)(2,1)} %bitcast.33) | data formatting | bytes 1835008
  33.4 0.0 copy-done.1
  33.4 0.0 copy-start
  33.4 0.9 %copy.18 = f32[16,2,7168]{2,1,0:T(2,128)} copy(f32[16,2,7168]{2,1,0:T(2,128)S(1)} %bitcast.32) | data formatting | bytes 1835008
  34.3 0.6 %copy-done = f32[16,112,128]{2,1,0:T(8,128)S(1)} copy-done((f32[16,112,128]{2,1,0:T(8,128)S(1)}, f32[16,112,128]{2,1,0:T(8,128)}, u32[]{:S(2)}) %copy-start) | copy-done | bytes 917528
  34.9 0.9 %copy.19 = f32[16,2,7168]{2,1,0:T(2,128)} copy(f32[16,2,7168]{2,1,0:T(2,128)S(1)} %bitcast.31) | data formatting | bytes 1835008
Async XLA Ops:
  30.6 2.8 %copy-start.1 = (f32[16,112,128]{2,1,0:T(8,128)S(1)}, f32[16,112,128]{2,1,0:T(8,128)}, u32[]{:S(2)}) copy-start(f32[16,112,128]{2,1,0:T(8,128)} %get-tuple-element.7) | copy-start | bytes 2752516
  33.4 1.5 %copy-start = (f32[16,112,128]{2,1,0:T(8,128)S(1)}, f32[16,112,128]{2,1,0:T(8,128)}, u32[]{:S(2)}) copy-start(f32[16,112,128]{2,1,0:T(8,128)} %get-tuple-element.8) | copy-start | bytes 2752516

commit v2 on v1

--- a/solution.py
+++ b/solution.py
@@ -28,22 +28,18 @@
     master_params,
     first_moment,
     second_moment,
-    out_params,
-    out_first,
-    out_second,
+    params,
+    new_first,
+    new_second,
     master,
     first,
     second,
-    params,
-    new_first,
-    new_second,
     order,
     slots,
     places,
     load_sem,
     state_sem,
     own_sem,
-    store_sem,
     y_send,
     y_recv,
     z_send,
@@ -108,11 +104,6 @@
             device_id_type=MESH,
         )
 
-    def store(c, which):
-        held, out = ((new_first, out_first), (new_second, out_second))[which]
-        part = pl.ds(starts[c] * rows, chunks[c] * rows)
-        return pltpu.make_async_copy(held.at[:, part], out.at[:, part], store_sem.at[c, which])
-
     barrier = pltpu.get_barrier_semaphore()
     axes = (("replica", my_replica, replicas), ("expert", my_expert, experts), ("tensor", my_tensor, tensors))
     for axis, mine, size in axes:
@@ -236,8 +227,6 @@
         adam(c)
         for d in range(1, tensors):
             x_copy(c, d).start()
-        for which in range(2):
-            store(c, which).start()
 
     for c in range(count):
         add_up(c)
@@ -254,14 +243,22 @@
             y_copy(c, d).wait_send()
         for d in range(1, experts):
             z_copy(c, d).wait_send()
-        for which in range(2):
-            store(c, which).wait()
     for c in range(count):
         for d in range(1, tensors):
             x_copy(c, d).wait()
-    last = pltpu.make_async_copy(params, out_params, state_sem.at[0])
-    last.start()
-    last.wait()
+
+
+def write_out(*refs):
+    half = (len(refs) - 1) // 2
+    sems = refs[-1]
+    copies = [
+        pltpu.make_async_copy(refs[i], refs[half + i], sems.at[i])
+        for i in range(half)
+    ]
+    for copy in copies:
+        copy.start()
+    for copy in copies:
+        copy.wait()
 
 
 def body(delta, step_offsets, block_map, master_params, first_moment, second_moment, *, shape):
@@ -284,24 +281,22 @@
 
     state_shape = (blocks, columns * rows, LANES)
     params_shape = (blocks, tensors * columns, rows, LANES)
-    anywhere = pl.BlockSpec(memory_space=pl.ANY)
+    anywhere = pl.BlockSpec(memory_space=pltpu.HBM)
+    near = pl.BlockSpec(memory_space=pltpu.VMEM)
     scalars = pl.BlockSpec(memory_space=pltpu.SMEM)
     dma = pltpu.SemaphoreType.DMA
     sizes = (replicas, experts, tensors, chunks, blocks, pairs, rows)
-    new_params, new_first, new_second = pl.pallas_call(
+    held = pl.pallas_call(
         functools.partial(kernel, sizes),
         out_shape=(
-            jax.ShapeDtypeStruct(params_shape, jnp.bfloat16),
-            jax.ShapeDtypeStruct(state_shape, jnp.float32),
-            jax.ShapeDtypeStruct(state_shape, jnp.float32),
+            pltpu.VMEM(params_shape, jnp.bfloat16),
+            pltpu.VMEM(state_shape, jnp.float32),
+            pltpu.VMEM(state_shape, jnp.float32),
         ),
         in_specs=[scalars] * 2 + [anywhere] * 4,
-        out_specs=(anywhere,) * 3,
+        out_specs=(near,) * 3,
         scratch_shapes=[
             pltpu.VMEM(state_shape, jnp.float32),
-            pltpu.VMEM(state_shape, jnp.float32),
-            pltpu.VMEM(state_shape, jnp.float32),
-            pltpu.VMEM(params_shape, jnp.bfloat16),
             pltpu.VMEM(state_shape, jnp.float32),
             pltpu.VMEM(state_shape, jnp.float32),
             pltpu.SMEM((blocks,), jnp.int32),
@@ -310,7 +305,6 @@
             dma((count, replicas)),
             dma((3,)),
             dma((count,)),
-            dma((count, 2)),
             dma((count, replicas)),
             dma((count, replicas)),
             dma((count, experts)),
@@ -324,6 +318,18 @@
         + [pltpu.VMEM((blocks, c, rows, LANES), jnp.bfloat16) for c in chunks],
         compiler_params=pltpu.CompilerParams(collective_id=0, has_side_effects=True),
     )(block_map, step_offsets, terms, dense(master_params), dense(first_moment), dense(second_moment))
+    new_params, new_first, new_second = pl.pallas_call(
+        write_out,
+        out_shape=(
+            jax.ShapeDtypeStruct(params_shape, jnp.bfloat16),
+            jax.ShapeDtypeStruct(state_shape, jnp.float32),
+            jax.ShapeDtypeStruct(state_shape, jnp.float32),
+        ),
+        in_specs=[near] * 3,
+        out_specs=(anywhere,) * 3,
+        scratch_shapes=[dma((3,))],
+        compiler_params=pltpu.CompilerParams(vmem_limit_bytes=1024 * 1024),
+    )(*held)
     full = new_params.transpose(0, 2, 1, 3).reshape(blocks, rows, tensors * width)
     return (full, undense(new_first), undense(new_second))
 

time: 36 us -> 31.2 us (0.87)
  local copies, waits for them, and re-layouts: 5.25 us -> 0 us
  Pallas kernels: 29.9 us -> 30.4 us
    unnamed x7 -> x0, local copies, waits for them, and re-layouts: 5.25 us -> none
    pallas_call x1 -> x2, Pallas kernels: 29.9 us -> 30.4 us  [the longest x1 28.9 us: body(): pl.pallas_call(functools.partial(kernel, sizes), out_shape=(pltpu.VMEM(pa...]
where the time goes in v2:
time: 31.2 us; the launch traced here: 31.1 us
  Pallas kernels  30.4 us (97%)
  between operations  0.64 us (2%)
    pallas_call x1, Pallas kernels, body(): pl.pallas_call(functools.partial(kernel, sizes), out_shape=(pltpu.VMEM(pa...  28.9 us
    pallas_call x1, Pallas kernels, body(): pl.pallas_call(write_out, out_shape=(jax.ShapeDtypeStruct(params_shape, j...  1.56 us

profile of v2, /device:TPU:0, one launch (start us, length us, event | category | flops | bytes accessed | tf_op | source)
XLA Modules:
  0.0 31.1 jit_solution(3639023847943020022)
XLA Ops:
  0.6 28.9 %shard_map.85 = (bf16[16,112,2,128]{3,2,1,0:T(2,128)(2,1)S(1)}, f32[16,112,128]{2,1,0:T(8,128)S(1)}, f32[16,112,128]{2,1,0:T(8,128)S(1)}) custom-call(s32[128]{0:T(128)} %block_map.1, s32[2]{0:T(128)} %step_offsets.1, bf16[16,56,2,2,128]{4,3,2,1,0:T(2,128)(2,1)} %bitcast.31, f32[16,112,128]{2,1,0:T(8,128)} %bitcast.32, f32[16,112,128]{2,1,0:T(8,128)} %bitcast.33, ...), custom_call_target="tpu_custom_call" | custom-call | tf_op jit(solution)/shard_map/pallas_call | solution.py:289
  29.5 1.6 %shard_map.86 = (bf16[16,112,2,128]{3,2,1,0:T(2,128)(2,1)}, f32[16,112,128]{2,1,0:T(8,128)}, f32[16,112,128]{2,1,0:T(8,128)}) custom-call(bf16[16,112,2,128]{3,2,1,0:T(2,128)(2,1)S(1)} %get-tuple-element.9.refs_0_, f32[16,112,128]{2,1,0:T(8,128)S(1)} %get-tuple-element.10.refs_1_, f32[16,112,128]{2,1,0:T(8,128)S(1)} %get-tuple-element.11.refs_2_), custom_call_target="tpu_custom_call" | custom-call | tf_op jit(solution)/shard_map/pallas_call | solution.py:321

commit v3 on v2

--- a/solution.py
+++ b/solution.py
@@ -15,8 +15,8 @@
 
 LANES = 128
 CHUNK = 8
-LAG = 3
-UNROLL = 4
+LAG = 2
+UNROLL = 16
 MESH = pl.DeviceIdType.MESH
 
 

time: 31.2 us -> 30.9 us (level)
  no operation moved by 1% of the time
where the time goes in v3:
time: 30.9 us; the launch traced here: 30.8 us
  Pallas kernels  30.1 us (97%)
  between operations  0.64 us (2%)
    pallas_call x1, Pallas kernels, body(): pl.pallas_call(functools.partial(kernel, sizes), out_shape=(pltpu.VMEM(pa...  28.6 us
    pallas_call x1, Pallas kernels, body(): pl.pallas_call(write_out, out_shape=(jax.ShapeDtypeStruct(params_shape, j...  1.56 us

profile of v3, /device:TPU:0, one launch (start us, length us, event | category | flops | bytes accessed | tf_op | source)
XLA Modules:
  0.0 30.8 jit_solution(13070434902727717776)
XLA Ops:
  0.6 28.6 %shard_map.85 = (bf16[16,112,2,128]{3,2,1,0:T(2,128)(2,1)S(1)}, f32[16,112,128]{2,1,0:T(8,128)S(1)}, f32[16,112,128]{2,1,0:T(8,128)S(1)}) custom-call(s32[128]{0:T(128)} %block_map.1, s32[2]{0:T(128)} %step_offsets.1, bf16[16,56,2,2,128]{4,3,2,1,0:T(2,128)(2,1)} %bitcast.31, f32[16,112,128]{2,1,0:T(8,128)} %bitcast.32, f32[16,112,128]{2,1,0:T(8,128)} %bitcast.33, ...), custom_call_target="tpu_custom_call" | custom-call | tf_op jit(solution)/shard_map/pallas_call | solution.py:289
  29.2 1.6 %shard_map.86 = (bf16[16,112,2,128]{3,2,1,0:T(2,128)(2,1)}, f32[16,112,128]{2,1,0:T(8,128)}, f32[16,112,128]{2,1,0:T(8,128)}) custom-call(bf16[16,112,2,128]{3,2,1,0:T(2,128)(2,1)S(1)} %get-tuple-element.9.refs_0_, f32[16,112,128]{2,1,0:T(8,128)S(1)} %get-tuple-element.10.refs_1_, f32[16,112,128]{2,1,0:T(8,128)S(1)} %get-tuple-element.11.refs_2_), custom_call_target="tpu_custom_call" | custom-call | tf_op jit(solution)/shard_map/pallas_call | solution.py:321
